TPU v7x, 32 devices: a whole 2x2x4 slice. The times are simulated.
32 devices in a mesh: tenant: 2 (over y), ctx: 2 (over x), head: 8 (over z, core).
Axes of the slice: x: 2, y: 2, z: 4, core: 2. Of those that a mesh axis runs over, the one named last changes fastest.
Arguments:
- tokens: bfloat16 [1024, 4608], P(('tenant', 'ctx'), 'head'), parts along dimension 0, may hold values from -6 to 6
- query_frozen_matrix: bfloat16 [4608, 2048], P('ctx', 'head'), may hold values from -0.09375 to 0.09375
- key_weight: bfloat16 [4608, 1024], P('ctx', 'head'), may hold values from -0.09375 to 0.09375
- value_frozen_matrix: bfloat16 [4608, 1024], P('ctx', 'head'), may hold values from -0.09375 to 0.09375
- query_down: bfloat16 [9216, 16], P('tenant'), parts along dimension 0, may hold values from -0.09375 to 0.09375
- query_adapter_expand: bfloat16 [32, 2048], P('tenant', 'head'), parts along dimension 0, may hold values from -1.5 to 1.5
- value_down: bfloat16 [9216, 16], P('tenant'), parts along dimension 0, may hold values from -0.09375 to 0.09375
- value_adapter_expand: bfloat16 [32, 1024], P('tenant', 'head'), parts along dimension 0, may hold values from -1.5 to 1.5
- block_order: int32 [8], P('tenant'), parts along dimension 0, may hold values from 0 to 3, each once
- doc_starts: int32 [24], P('tenant'), parts along dimension 0, may hold values from 0 to 511, as said below
- prompt_of: int32 [24], P('tenant'), parts along dimension 0, may hold values from 0 to 11, as said below
Outputs:
- attended: bfloat16 [1024, 2048], P(('tenant', 'ctx'), 'head'), parts along dimension 0
There are 2 independent parts, one for each index of `tenant`. A program takes and returns all parts, laid end to end along the dimension named above; an argument that names none is the same for every part. Nothing has to cross between parts.
Inputs may be any that keep to these rules, and one draw needn't show every extreme that they name: `doc_starts`: strictly increasing with first entry 0; the segments come in 4 groups of three: a prompt, a chosen and a rejected response. `prompt_of`: for segment j = 3k it is j; for j = 3k + 1 it is 3k; for j = 3k + 2 it is 3k or j. `block_order`: each of 0 to 3 once.
All inputs are finite; a program needn't handle non-finite values.
Results may differ from a plain program's by a relative error of at most 0.012.
Values may be sent and summed in bfloat16 or wider, within the bound.
No kernel may reach another device: no remote copies, remote signals or barrier semaphores. Data moves between devices by JAX's collectives and lax.ppermute only.
A program may use at most 64 MiB of HBM per device.

v0:
```python
import math
import jax
import jax.numpy as jnp
from jax import lax
from jax.sharding import PartitionSpec as P

HD = 128
softcap_limit = 50.0
query_scale = 144.0 ** (-0.5)
adapter_scaling = 2.0
rope_base = 10000.0


def row_meta(row_ids, block_order, doc_starts, prompt_of, block_len, sequence_len):
    block_count = block_order.shape[0]
    block_id = row_ids // block_len
    one_hot = block_id[:, None] == jnp.arange(block_count, dtype=jnp.int32)[None, :]
    ordered = jnp.sum(jnp.where(one_hot, block_order[None, :], 0), axis=1)
    places = ordered * block_len + row_ids % block_len
    segment = jnp.sum((doc_starts[None, :] <= places[:, None]).astype(jnp.int32), axis=1) - 1
    seg_ids = jnp.arange(doc_starts.shape[0], dtype=jnp.int32)
    selected = segment[:, None] == seg_ids[None, :]
    prompt_seg = jnp.sum(jnp.where(selected, prompt_of[None, :], 0), axis=1)
    own_start = jnp.sum(jnp.where(selected, doc_starts[None, :], 0), axis=1)
    next_starts = jnp.concatenate([doc_starts[1:], jnp.full((1,), sequence_len, jnp.int32)])
    prompt_sel = prompt_seg[:, None] == seg_ids[None, :]
    prompt_len = jnp.sum(jnp.where(prompt_sel, (next_starts - doc_starts)[None, :], 0), axis=1)
    rotary_pos = places - own_start + jnp.where(prompt_seg != segment, prompt_len, 0)
    return (places, segment, prompt_seg, rotary_pos)


def rotate(values_in, rotary_pos):
    width_half = values_in.shape[-1] // 2
    frequency = jnp.exp(
        jnp.arange(width_half, dtype=jnp.float32)
        * (-2.0 * math.log(rope_base) / values_in.shape[-1])
    )
    angles = rotary_pos.astype(jnp.float32)[:, None] * frequency[None, :]
    cosine = jnp.concatenate([jnp.cos(angles), jnp.cos(angles)], axis=-1)[:, None, :]
    sine_part = jnp.concatenate([jnp.sin(angles), jnp.sin(angles)], axis=-1)[:, None, :]
    rotated = jnp.concatenate([-values_in[..., width_half:], values_in[..., :width_half]], axis=-1)
    return values_in * cosine + rotated * sine_part


def visible_mask(query_info, key_info):
    same_doc = (key_info[1][None, :] == query_info[1][:, None]) & (
        key_info[0][None, :] <= query_info[0][:, None]
    )
    from_prompt = (key_info[1][None, :] == query_info[2][:, None]) & (
        query_info[2] != query_info[1]
    )[:, None]
    return same_doc | from_prompt


def local(
    tokens,
    query_frozen_matrix,
    key_weight,
    value_frozen_matrix,
    query_down,
    query_adapter_expand,
    value_down,
    value_adapter_expand,
    block_order,
    doc_starts,
    prompt_of,
):
    tok_rows = tokens.shape[0]
    cycle_size = lax.axis_size("ctx")
    device = lax.axis_index("ctx")
    sequence_len = tok_rows * cycle_size
    block_len = tok_rows // 2
    full_tokens = lax.all_gather(tokens, "head", axis=1, tiled=True)

    def add_rows(weight_part):
        return jnp.dot(full_tokens, weight_part, preferred_element_type=jnp.float32)

    frozen_query_output = add_rows(lax.all_gather(query_frozen_matrix, "ctx", axis=0, tiled=True))
    key_base = add_rows(lax.all_gather(key_weight, "ctx", axis=0, tiled=True))
    frozen_value_output = add_rows(lax.all_gather(value_frozen_matrix, "ctx", axis=0, tiled=True))
    own_ids = device * tok_rows + jnp.arange(tok_rows, dtype=jnp.int32)
    own_info = row_meta(own_ids, block_order, doc_starts, prompt_of, block_len, sequence_len)
    local_heads = query_frozen_matrix.shape[1] // HD
    local_kv = key_weight.shape[1] // HD
    per_kv = local_heads // local_kv
    query_adapter_hidden = jnp.dot(
        full_tokens, query_down, preferred_element_type=jnp.float32
    ).astype(jnp.bfloat16)
    query_states = frozen_query_output + adapter_scaling * jnp.dot(
        query_adapter_hidden, query_adapter_expand, preferred_element_type=jnp.float32
    )
    query_states = (
        rotate(query_states.reshape(tok_rows, local_heads, HD), own_info[3]) * query_scale
    ).astype(jnp.bfloat16)
    query_heads = query_states.reshape(tok_rows, local_kv, per_kv, HD)
    key_proj = (
        rotate(key_base.reshape(tok_rows, local_kv, HD), own_info[3])
        .astype(jnp.bfloat16)
        .reshape(tok_rows, local_kv * HD)
    )
    value_adapter_hidden = jnp.dot(
        full_tokens, value_down, preferred_element_type=jnp.float32
    ).astype(jnp.bfloat16)
    value_projected = (
        frozen_value_output
        + adapter_scaling
        * jnp.dot(value_adapter_hidden, value_adapter_expand, preferred_element_type=jnp.float32)
    ).astype(jnp.bfloat16)
    pieces = (
        lax.all_gather(key_proj, "ctx", axis=0, tiled=True),
        lax.all_gather(value_projected, "ctx", axis=0, tiled=True),
    )
    key_ids = jnp.arange(pieces[0].shape[0], dtype=jnp.int32)
    key_block = pieces[0]
    value_block = pieces[1]
    key_info = row_meta(key_ids, block_order, doc_starts, prompt_of, block_len, sequence_len)
    visible = visible_mask(own_info, key_info)
    key_heads = key_block.reshape(key_block.shape[0], local_kv, HD)
    value_heads = value_block.reshape(value_block.shape[0], local_kv, HD)
    scores = jnp.einsum(
        "tkgd,skd->kgts", query_heads, key_heads, preferred_element_type=jnp.float32
    )
    capped = softcap_limit * jnp.tanh(scores / softcap_limit)
    unnorm = jnp.where(visible[None, None], jnp.exp(capped), jnp.zeros_like(capped))
    denominator = jnp.sum(unnorm, axis=-1)
    numerator = jnp.einsum(
        "kgts,skd->tkgd",
        unnorm.astype(jnp.bfloat16),
        value_heads,
        preferred_element_type=jnp.float32,
    )
    numerator, denominator = (numerator, denominator)
    attended = numerator / jnp.transpose(denominator, (2, 0, 1))[..., None]
    return attended.reshape(tok_rows, local_heads * HD).astype(jnp.bfloat16)


def solution(mesh):
    in_specs = (
        P(("tenant", "ctx"), "head"),
        P("ctx", "head"),
        P("ctx", "head"),
        P("ctx", "head"),
        P("tenant", None),
        P("tenant", "head"),
        P("tenant", None),
        P("tenant", "head"),
        P("tenant"),
        P("tenant"),
        P("tenant"),
    )
    out_specs = P(("tenant", "ctx"), "head")
    return jax.shard_map(local, mesh=mesh, in_specs=in_specs, out_specs=out_specs, check_vma=False)
```

profile of v0, /device:TPU:0, one launch (start us, length us, event | category | flops | bytes accessed | tf_op | source)
XLA Modules:
  0.0 143.6 jit_solution(536576771758366168)
XLA Ops:
  6.5 0.0 all-gather.9.cloned.1.call-start
  6.6 0.7 all-gather.9.cloned.1.call-update
  7.3 0.0 all-gather.5.cloned.1.call-start
  7.3 0.7 all-gather.5.cloned.1.call-update
  8.0 0.0 all-gather.11.cloned.1.call-start
  8.1 0.7 all-gather.11.cloned.1.call-update
  8.8 0.0 all-gather.7.cloned.1.call-start
  8.8 0.5 all-gather.7.cloned.1.call-update
  9.4 0.1 slice.15
  9.5 0.1 select_reduce_fusion.4
  9.6 0.1 convert_reduce_fusion.1
  9.7 0.1 select_reduce_fusion.3
  9.7 0.1 convert_reduce_fusion
  9.8 0.1 add_subtract_fusion
  9.9 0.1 select_reduce_fusion.1
  10.0 0.1 select_reduce_fusion
  10.1 0.3 multiply_cosine_fusion
  10.4 0.2 and_or_fusion
  10.7 23.7 %all-gather.9.cloned.1.call-done = bf16[4608,128]{1,0:T(8,128)(2,1)} async-done(((bf16[2304,128]{1,0:T(8,128)(2,1)}), bf16[4608,128]{1,0:T(8,128)(2,1)}) %all-gather.9.cloned.1.call-update) | async-done | bytes 1179664 | tf_op jit(solution)/shard_map/all_gather | solution.py:79
  34.4 33.1 %all-gather.5.cloned.1.call-done = bf16[256,4608]{0,1:T(8,128)(2,1)} async-done(((bf16[256,576]{0,1:T(8,128)(2,1)}), bf16[256,4608]{0,1:T(8,128)(2,1)}) %all-gather.5.cloned.1.call-update) | async-done | bytes 2359312 | tf_op jit(solution)/shard_map/all_gather | solution.py:73
  67.5 2.7 %fusion.30 = f32[256,128]{0,1:T(8,128)S(1)} fusion(bf16[256,4608]{0,1:T(8,128)(2,1)} %all-gather.5.cloned.1.call-done, bf16[4608,128]{1,0:T(8,128)(2,1)} %all-gather.9.cloned.1.call-done), kind=kOutput, calls=%fused_computation.76 | convolution fusion | flops 301989888 | bytes 3670016 | tf_op jit(solution)/shard_map/dot_general | solution.py:76
  70.4 4.9 %all_gather.22 = bf16[512,128]{0,1:T(8,128)(2,1)S(1)} all-gather(bf16[256,128]{0,1:T(8,128)(2,1)S(1)} %get-tuple-element.13), channel_id=1, replica_groups=mesh['tenant'=2,'ctx'=2,'head'=8] {'ctx'}, dimensions={0}, use_global_device_ids=true | all-gather | bytes 196608 | tf_op jit(solution)/shard_map/all_gather | solution.py:110
  75.3 1.0 convolution_multiply_fusion.1
  76.3 28.1 %all-gather.11.cloned.1.call-done = bf16[4608,256]{1,0:T(8,128)(2,1)} async-done(((bf16[2304,256]{1,0:T(8,128)(2,1)}), bf16[4608,256]{1,0:T(8,128)(2,1)}) %all-gather.11.cloned.1.call-update) | async-done | bytes 2359312 | tf_op jit(solution)/shard_map/all_gather | solution.py:78
  104.4 2.7 %convolution_add_fusion = f32[256,256]{0,1:T(8,128)S(1)} fusion(f32[256,256]{0,1:T(8,128)S(1)} %convolution_multiply_fusion.1, bf16[256,4608]{0,1:T(8,128)(2,1)S(1)} %copy-done.4, bf16[4608,256]{1,0:T(8,128)(2,1)} %all-gather.11.cloned.1.call-done), kind=kOutput, calls=%fused_computation.7 | convolution fusion | flops 604045312 | bytes 5242880 | tf_op jit(solution)/shard_map/dot_general | solution.py:76
  107.1 2.5 %convolution_multiply_fusion.2 = f32[256,128]{0,1:T(8,128)} fusion(bf16[16,128]{1,0:T(8,128)(2,1)} %param.18, bf16[256,4608]{0,1:T(8,128)(2,1)S(1)} %copy-done.4, bf16[4608,16]{0,1:T(8,128)(2,1)} %param.17), kind=kOutput, calls=%fused_computation.10 | convolution fusion | flops 38834176 | bytes 2641920 | tf_op jit(solution)/shard_map/dot_general | solution.py:107
  109.7 18.9 %all-gather.7.cloned.1.call-done = bf16[4608,128]{1,0:T(8,128)(2,1)} async-done(((bf16[2304,128]{1,0:T(8,128)(2,1)}), bf16[4608,128]{1,0:T(8,128)(2,1)}) %all-gather.7.cloned.1.call-update) | async-done | bytes 1179664 | tf_op jit(solution)/shard_map/all_gather | solution.py:80
  128.6 1.9 %fusion.5 = bf16[256,128]{0,1:T(8,128)(2,1)S(1)} fusion(f32[256,128]{0,1:T(8,128)} %convolution_multiply_fusion.2, bf16[256,4608]{0,1:T(8,128)(2,1)S(1)} %copy-done.4, bf16[4608,128]{1,0:T(8,128)(2,1)} %all-gather.7.cloned.1.call-done), kind=kOutput, calls=%fused_computation.11 | convolution fusion | flops 302055424 | bytes 3735552 | tf_op jit(solution)/shard_map/dot_general | solution.py:76
  130.5 4.9 %all_gather.20 = bf16[512,128]{0,1:T(8,128)(2,1)S(1)} all-gather(bf16[256,128]{0,1:T(8,128)(2,1)S(1)} %fusion.5), channel_id=1, replica_groups=mesh['tenant'=2,'ctx'=2,'head'=8] {'ctx'}, dimensions={0}, use_global_device_ids=true | all-gather | bytes 196608 | tf_op jit(solution)/shard_map/all_gather | solution.py:111
  135.5 0.5 fusion.29
  136.0 0.2 fusion.7
  136.3 0.8 copy.19
  (25 shorter events, 0.2 us)
Async XLA Ops:
  6.5 68.8 %copy-start = (bf16[4608,16]{0,1:T(8,128)(2,1)S(1)}, bf16[4608,16]{0,1:T(8,128)(2,1)}, u32[]{:S(2)}) copy-start(bf16[4608,16]{0,1:T(8,128)(2,1)} %param.15) | copy-start | bytes 442372
  6.5 2.8 %copy-start.1 = (s32[12]{0:T(128)S(1)}, s32[12]{0:T(128)}, u32[]{:S(2)}) copy-start(s32[12]{0:T(128)} %param.20) | copy-start | bytes 148
  6.5 2.9 %copy-start.2 = (s32[4]{0:T(128)S(1)}, s32[4]{0:T(128)}, u32[]{:S(2)}) copy-start(s32[4]{0:T(128)} %param.19) | copy-start | bytes 52
  6.5 3.4 %copy-start.3 = (s32[12]{0:T(128)S(1)}, s32[12]{0:T(128)}, u32[]{:S(2)}) copy-start(s32[12]{0:T(128)} %param.21) | copy-start | bytes 148
  6.5 27.9 %all-gather.9.cloned.1.call-start = ((), (), s32[]{:S(2)}) async-start(), calls=%async_computation.2 | async-start | bytes 1769472 | tf_op jit(solution)/shard_map/all_gather | solution.py:79
  7.3 60.3 %all-gather.5.cloned.1.call-start = ((), (), s32[]{:S(2)}) async-start(), calls=%async_computation | async-start | bytes 2654208 | tf_op jit(solution)/shard_map/all_gather | solution.py:73
  8.0 96.4 %all-gather.11.cloned.1.call-start = ((), (), s32[]{:S(2)}) async-start(), calls=%async_computation.3 | async-start | bytes 3538944 | tf_op jit(solution)/shard_map/all_gather | solution.py:78
  8.8 119.8 %all-gather.7.cloned.1.call-start = ((), (), s32[]{:S(2)}) async-start(), calls=%async_computation.1 | async-start | bytes 1769472 | tf_op jit(solution)/shard_map/all_gather | solution.py:80
  10.7 64.6 %copy-start.5 = (bf16[16,256]{1,0:T(8,128)(2,1)S(1)}, bf16[16,256]{1,0:T(8,128)(2,1)}, u32[]{:S(2)}) copy-start(bf16[16,256]{1,0:T(8,128)(2,1)} %param.16) | copy-start | bytes 24580
  67.5 7.8 %copy-start.4 = (bf16[256,4608]{0,1:T(8,128)(2,1)S(1)}, bf16[256,4608]{0,1:T(8,128)(2,1)}, u32[]{:S(2)}) copy-start(bf16[256,4608]{0,1:T(8,128)(2,1)} %all-gather.5.cloned.1.call-done) | copy-start | bytes 7077892
Sparse Core Ops, SparseCore 0:
  8.9 25.4 all-gather.8
  36.1 31.4 all-gather.4
  69.1 35.2 all-gather.10
  105.8 22.7 all-gather.6
where the time goes:
time: 144 us
  waiting for transfers between devices  106 us (74%)
  between operations  13.3 us (9%)
  matrix products  11.6 us (8%)
  blocking collectives  9.87 us (7%)
    all_gather x1, waiting for transfers between devices, local(): full_tokens = lax.all_gather(tokens, 'head', axis=1, tiled=True)  33.1 us
    all_gather x1, waiting for transfers between devices, local(): lax.all_gather(query_frozen_matrix, 'ctx', axis=0, tiled=True)  28.1 us
    all_gather x1, waiting for transfers between devices, local(): key_base = add_rows(lax.all_gather(key_weight, 'ctx', axis=0, tiled=True))  23.7 us
    all_gather x1, waiting for transfers between devices, local(): lax.all_gather(value_frozen_matrix, 'ctx', axis=0, tiled=True)  18.9 us
    dot_general x3, matrix products, add_rows(): return jnp.dot(full_tokens, weight_part, preferred_element_type=jnp.float32)  7.33 us
    all_gather x1, blocking collectives, local(): lax.all_gather(key_proj, 'ctx', axis=0, tiled=True)  4.93 us
    all_gather x1, blocking collectives, local(): lax.all_gather(value_projected, 'ctx', axis=0, tiled=True)  4.93 us
  transfers between devices with their start and end apart: 4, of which 4 were waited for; matrix products, arithmetic and copies ran while one was open for 7% of the time, Pallas kernels for 0%

commit v1 on v0

--- a/solution.py
+++ b/solution.py
@@ -9,6 +9,12 @@
 query_scale = 144.0 ** (-0.5)
 adapter_scaling = 2.0
 rope_base = 10000.0
+
+
+def laid_out(blocks, dim):
+    blocks = jnp.moveaxis(blocks, 0, dim)
+    shape = blocks.shape
+    return blocks.reshape(*shape[:dim], shape[dim] * shape[dim + 1], *shape[dim + 2 :])
 
 
 def row_meta(row_ids, block_order, doc_starts, prompt_of, block_len, sequence_len):
@@ -70,7 +76,14 @@
     device = lax.axis_index("ctx")
     sequence_len = tok_rows * cycle_size
     block_len = tok_rows // 2
-    full_tokens = lax.all_gather(tokens, "head", axis=1, tiled=True)
+    size = lax.axis_size("head")
+    right = [(i, (i + 1) % size) for i in range(size)]
+    pieces_2 = [tokens]
+    while len(pieces_2) < size:
+        pieces_2.append(lax.ppermute(pieces_2[-1], "head", right))
+    index = lax.axis_index("head")
+    pieces_2 = jnp.stack(pieces_2)[(index - jnp.arange(size)) % size]
+    full_tokens = laid_out(pieces_2, 1)
 
     def add_rows(weight_part):
         return jnp.dot(full_tokens, weight_part, preferred_element_type=jnp.float32)

time: 144 us -> 110 us (0.76)
  waiting for transfers between devices: 106 us -> 66.4 us
  blocking collectives: 9.87 us -> 13.3 us
  local copies, waits for them, and re-layouts: 0.86 us -> 3.15 us
    ppermute x0 -> x7, waiting for transfers between devices: none -> 54.6 us  [local(): pieces_2.append(lax.ppermute(pieces_2[-1], 'head', right))]
    all_gather x1 -> x0, waiting for transfers between devices: 33.1 us -> none  [local(): full_tokens = lax.all_gather(tokens, 'head', axis=1, tiled=True)]
    all_gather x1, waiting for transfers between devices: 23.7 us -> 0.01 us  [local(): key_base = add_rows(lax.all_gather(key_weight, 'ctx', axis=0, tiled=True))]
    all_gather x1, waiting for transfers between devices: 18.9 us -> 0.02 us  [local(): lax.all_gather(value_frozen_matrix, 'ctx', axis=0, tiled=True)]
    all_gather x1, waiting for transfers between devices: 28.1 us -> 10.3 us  [local(): lax.all_gather(query_frozen_matrix, 'ctx', axis=0, tiled=True)]
    gather x0 -> x1, local copies, waits for them, and re-layouts: none -> 2.12 us  [local(): pieces_2 = jnp.stack(pieces_2)[(index - jnp.arange(size)) % size]]
    all_gather x1, blocking collectives: 4.93 us -> 6.87 us  [local(): lax.all_gather(key_proj, 'ctx', axis=0, tiled=True)]
    dot_general x1, matrix products: 2.53 us -> 0.96 us  [local(): jnp.dot(value_adapter_hidden, value_adapter_expand, preferred_element_typ...]
  transfers between devices with their start and end apart: 4 -> 10, of which waited for: 4 -> 8; matrix products, arithmetic and copies ran while one was open for 7% -> 10% of each run, Pallas kernels for 0% -> 0%
where the time goes in v1:
time: 110 us; the launch traced here: 109 us
  waiting for transfers between devices  66.4 us (60%)
  blocking collectives  13.3 us (12%)
  between operations  13.3 us (12%)
  matrix products  11.1 us (10%)
  local copies, waits for them, and re-layouts  3.15 us (3%)
  other arithmetic  1.39 us (1%)
    ppermute x7, waiting for transfers between devices, local(): pieces_2.append(lax.ppermute(pieces_2[-1], 'head', right))  54.6 us
    all_gather x1, waiting for transfers between devices, local(): lax.all_gather(query_frozen_matrix, 'ctx', axis=0, tiled=True)  10.3 us
    dot_general x3, matrix products, add_rows(): return jnp.dot(full_tokens, weight_part, preferred_element_type=jnp.float32)  7.68 us
    all_gather x1, blocking collectives, local(): lax.all_gather(key_proj, 'ctx', axis=0, tiled=True)  6.87 us
    all_gather x1, blocking collectives, local(): lax.all_gather(value_projected, 'ctx', axis=0, tiled=True)  6.46 us
  transfers between devices with their start and end apart: 10, of which 8 were waited for; matrix products, arithmetic and copies ran while one was open for 10% of the time, Pallas kernels for 0%

profile of v1, /device:TPU:0, one launch (start us, length us, event | category | flops | bytes accessed | tf_op | source)
XLA Modules:
  0.0 109.4 jit_solution(7638920419863888257)
XLA Ops:
  6.6 0.7 all-gather.6.cloned.1.call-update
  7.3 0.7 all-gather.4.cloned.1.call-update
  8.1 0.5 collective-permute-start
  8.6 0.1 all-gather.8.cloned.1.call-update
  8.9 0.1 select_reduce_fusion.4
  9.0 0.1 convert_reduce_fusion.1
  9.1 0.1 select_reduce_fusion.3
  9.2 0.1 convert_reduce_fusion
  9.3 0.1 add_subtract_fusion
  9.3 0.1 select_reduce_fusion.1
  9.4 0.1 select_reduce_fusion
  9.5 7.7 %collective-permute-done = bf16[256,576]{0,1:T(8,128)(2,1)S(1)} collective-permute-done((bf16[256,576]{0,1:T(8,128)(2,1)}, bf16[256,576]{0,1:T(8,128)(2,1)S(1)}, u32[]{:S(2)}, u32[]{:S(2)}) %collective-permute-start) | collective-permute-done | bytes 294944 | tf_op jit(solution)/shard_map/ppermute | solution.py:83
  17.3 0.3 multiply_cosine_fusion
  17.6 7.6 %collective-permute-done.1 = bf16[256,576]{0,1:T(8,128)(2,1)S(1)} collective-permute-done((bf16[256,576]{0,1:T(8,128)(2,1)S(1)}, bf16[256,576]{0,1:T(8,128)(2,1)S(1)}, u32[]{:S(2)}, u32[]{:S(2)}) %collective-permute-start.1) | collective-permute-done | bytes 294944 | tf_op jit(solution)/shard_map/ppermute | solution.py:83
  25.2 0.2 and_or_fusion
  25.5 7.7 %collective-permute-done.2 = bf16[256,576]{0,1:T(8,128)(2,1)S(1)} collective-permute-done((bf16[256,576]{0,1:T(8,128)(2,1)S(1)}, bf16[256,576]{0,1:T(8,128)(2,1)S(1)}, u32[]{:S(2)}, u32[]{:S(2)}) %collective-permute-start.2) | collective-permute-done | bytes 294944 | tf_op jit(solution)/shard_map/ppermute | solution.py:83
  33.2 7.9 %collective-permute-done.3 = bf16[256,576]{0,1:T(8,128)(2,1)S(1)} collective-permute-done((bf16[256,576]{0,1:T(8,128)(2,1)S(1)}, bf16[256,576]{0,1:T(8,128)(2,1)S(1)}, u32[]{:S(2)}, u32[]{:S(2)}) %collective-permute-start.3) | collective-permute-done | bytes 294944 | tf_op jit(solution)/shard_map/ppermute | solution.py:83
  41.2 7.9 %collective-permute-done.4 = bf16[256,576]{0,1:T(8,128)(2,1)S(1)} collective-permute-done((bf16[256,576]{0,1:T(8,128)(2,1)S(1)}, bf16[256,576]{0,1:T(8,128)(2,1)S(1)}, u32[]{:S(2)}, u32[]{:S(2)}) %collective-permute-start.4) | collective-permute-done | bytes 294944 | tf_op jit(solution)/shard_map/ppermute | solution.py:83
  49.1 7.9 %collective-permute-done.5 = bf16[256,576]{0,1:T(8,128)(2,1)S(1)} collective-permute-done((bf16[256,576]{0,1:T(8,128)(2,1)S(1)}, bf16[256,576]{0,1:T(8,128)(2,1)S(1)}, u32[]{:S(2)}, u32[]{:S(2)}) %collective-permute-start.5) | collective-permute-done | bytes 294944 | tf_op jit(solution)/shard_map/ppermute | solution.py:83
  57.1 7.9 %collective-permute-done.6 = bf16[256,576]{0,1:T(8,128)(2,1)S(1)} collective-permute-done((bf16[256,576]{0,1:T(8,128)(2,1)S(1)}, bf16[256,576]{0,1:T(8,128)(2,1)S(1)}, u32[]{:S(2)}, u32[]{:S(2)}) %collective-permute-start.6) | collective-permute-done | bytes 294944 | tf_op jit(solution)/shard_map/ppermute | solution.py:83
  65.0 2.1 %gather_fusion = bf16[8,256,576]{1,2,0:T(8,128)(2,1)} fusion(bf16[8,256,576]{1,2,0:T(8,128)(2,1)S(1)} %bitcast_dynamic-update-slice_fusion, s32[1024]{0:T(1024)S(1)} %pad_clamp_fusion), kind=kCustom, calls=%fused_computation | custom fusion | bytes 4718624 | tf_op jit(solution)/shard_map/gather | solution.py:85
  67.1 3.0 %fusion.32 = f32[256,128]{0,1:T(8,128)S(1)} fusion(bf16[256,4608]{0,1:T(8,128)(2,1)} %bitcast.82, bf16[4608,128]{1,0:T(8,128)(2,1)} %all-gather.6.cloned.1.call-done), kind=kOutput, calls=%fused_computation.92 | convolution fusion | flops 301989888 | bytes 3670016 | tf_op jit(solution)/shard_map/dot_general | solution.py:89
  70.2 6.9 %all_gather.18 = bf16[512,128]{0,1:T(8,128)(2,1)S(1)} all-gather(bf16[256,128]{0,1:T(8,128)(2,1)S(1)} %get-tuple-element.13), channel_id=1, replica_groups=mesh['tenant'=2,'ctx'=2,'head'=8] {'ctx'}, dimensions={0}, use_global_device_ids=true | all-gather | bytes 196608 | tf_op jit(solution)/shard_map/all_gather | solution.py:123
  77.1 1.0 convolution_multiply_fusion.2
  78.1 1.9 %fusion.5 = bf16[256,128]{0,1:T(8,128)(2,1)S(1)} fusion(f32[256,128]{0,1:T(8,128)S(1)} %convolution_multiply_fusion.2, bf16[256,4608]{0,1:T(8,128)(2,1)S(1)} %bitcast.84, bf16[4608,128]{1,0:T(8,128)(2,1)} %all-gather.4.cloned.1.call-done), kind=kOutput, calls=%fused_computation.12 | convolution fusion | flops 302055424 | bytes 3735552 | tf_op jit(solution)/shard_map/dot_general | solution.py:89
  80.0 6.5 %all_gather.16 = bf16[512,128]{0,1:T(8,128)(2,1)S(1)} all-gather(bf16[256,128]{0,1:T(8,128)(2,1)S(1)} %fusion.5), channel_id=1, replica_groups=mesh['tenant'=2,'ctx'=2,'head'=8] {'ctx'}, dimensions={0}, use_global_device_ids=true | all-gather | bytes 196608 | tf_op jit(solution)/shard_map/all_gather | solution.py:124
  86.5 1.7 %convolution_multiply_fusion.1 = f32[256,256]{0,1:T(8,128)} fusion(bf16[16,256]{1,0:T(8,128)(2,1)S(1)} %copy-done.7, bf16[256,4608]{0,1:T(8,128)(2,1)S(1)} %bitcast.85, bf16[4608,16]{0,1:T(8,128)(2,1)S(1)} %copy-done), kind=kOutput, calls=%fused_computation.9 | convolution fusion | flops 39915520 | bytes 2777088 | tf_op jit(solution)/shard_map/dot_general | solution.py:102
  88.2 10.3 %all-gather.8.cloned.1.call-done = bf16[4608,256]{1,0:T(8,128)(2,1)} async-done(((bf16[2304,256]{1,0:T(8,128)(2,1)}), bf16[4608,256]{1,0:T(8,128)(2,1)}) %all-gather.8.cloned.1.call-update) | async-done | bytes 2359312 | tf_op jit(solution)/shard_map/all_gather | solution.py:91
  98.5 2.7 %convolution_add_fusion = f32[256,256]{0,1:T(8,128)S(1)} fusion(f32[256,256]{0,1:T(8,128)} %convolution_multiply_fusion.1, bf16[256,4608]{0,1:T(8,128)(2,1)S(1)} %bitcast.86, bf16[4608,256]{1,0:T(8,128)(2,1)} %all-gather.8.cloned.1.call-done), kind=kOutput, calls=%fused_computation.8 | convolution fusion | flops 604045312 | bytes 5242880 | tf_op jit(solution)/shard_map/dot_general | solution.py:89
  101.3 0.5 fusion.31
  101.8 0.2 fusion.7
  102.1 0.8 copy.19
  (53 shorter events, 0.7 us)
Async XLA Ops:
  6.5 80.0 %copy-start = (bf16[4608,16]{0,1:T(8,128)(2,1)S(1)}, bf16[4608,16]{0,1:T(8,128)(2,1)}, u32[]{:S(2)}) copy-start(bf16[4608,16]{0,1:T(8,128)(2,1)} %param.15) | copy-start | bytes 442372
  6.5 26.6 %copy-start.2 = (bf16[256,576]{0,1:T(8,128)(2,1)S(1)}, bf16[256,576]{0,1:T(8,128)(2,1)}, u32[]{:S(2)}) copy-start(bf16[256,576]{0,1:T(8,128)(2,1)} %param.11) | copy-start | bytes 884740
  6.5 2.2 %copy-start.3 = (s32[12]{0:T(128)S(1)}, s32[12]{0:T(128)}, u32[]{:S(2)}) copy-start(s32[12]{0:T(128)} %param.20) | copy-start | bytes 148
  6.5 2.3 %copy-start.4 = (s32[4]{0:T(128)S(1)}, s32[4]{0:T(128)}, u32[]{:S(2)}) copy-start(s32[4]{0:T(128)} %param.19) | copy-start | bytes 52
  6.5 2.8 %copy-start.5 = (s32[12]{0:T(128)S(1)}, s32[12]{0:T(128)}, u32[]{:S(2)}) copy-start(s32[12]{0:T(128)} %param.21) | copy-start | bytes 148
  6.5 60.5 %all-gather.6.cloned.1.call-start = ((), (), s32[]{:S(2)}) async-start(), calls=%async_computation.1 | async-start | bytes 1769472 | tf_op jit(solution)/shard_map/all_gather | solution.py:92
  7.3 70.8 %all-gather.4.cloned.1.call-start = ((), (), s32[]{:S(2)}) async-start(), calls=%async_computation | async-start | bytes 1769472 | tf_op jit(solution)/shard_map/all_gather | solution.py:93
  8.0 90.4 %all-gather.8.cloned.1.call-start = ((), (), s32[]{:S(2)}) async-start(), calls=%async_computation.2 | async-start | bytes 3538944 | tf_op jit(solution)/shard_map/all_gather | solution.py:91
  8.1 9.2 %collective-permute-start = (bf16[256,576]{0,1:T(8,128)(2,1)}, bf16[256,576]{0,1:T(8,128)(2,1)S(1)}, u32[]{:S(2)}, u32[]{:S(2)}) collective-permute-start(bf16[256,576]{0,1:T(8,128)(2,1)} %param.11), channel_id=1, source_target_pairs={{0,1},{1,2},{2,3},{3,4},{4,5},{5,6},{6,7},{7,0},{8,9},{9,10},{10,1... | collective-permute-start | bytes 884744 | tf_op jit(solution)/shard_map/ppermute | solution.py:83
  17.3 7.9 %collective-permute-start.1 = (bf16[256,576]{0,1:T(8,128)(2,1)S(1)}, bf16[256,576]{0,1:T(8,128)(2,1)S(1)}, u32[]{:S(2)}, u32[]{:S(2)}) collective-permute-start(bf16[256,576]{0,1:T(8,128)(2,1)S(1)} %collective-permute-done), channel_id=1, source_target_pairs={{0,1},{1,2},{2,3},{3,4},{4,5},{5,6},{6,7},{7,0},{8,9},{9,10},{10,1... | collective-permute-start | bytes 884744 | tf_op jit(solution)/shard_map/ppermute | solution.py:83
  25.2 7.9 %collective-permute-start.2 = (bf16[256,576]{0,1:T(8,128)(2,1)S(1)}, bf16[256,576]{0,1:T(8,128)(2,1)S(1)}, u32[]{:S(2)}, u32[]{:S(2)}) collective-permute-start(bf16[256,576]{0,1:T(8,128)(2,1)S(1)} %collective-permute-done.1), channel_id=1, source_target_pairs={{0,1},{1,2},{2,3},{3,4},{4,5},{5,6},{6,7},{7,0},{8,9},{9,10},{10,1... | collective-permute-start | bytes 884744 | tf_op jit(solution)/shard_map/ppermute | solution.py:83
  33.2 7.9 %collective-permute-start.3 = (bf16[256,576]{0,1:T(8,128)(2,1)S(1)}, bf16[256,576]{0,1:T(8,128)(2,1)S(1)}, u32[]{:S(2)}, u32[]{:S(2)}) collective-permute-start(bf16[256,576]{0,1:T(8,128)(2,1)S(1)} %collective-permute-done.2), channel_id=1, source_target_pairs={{0,1},{1,2},{2,3},{3,4},{4,5},{5,6},{6,7},{7,0},{8,9},{9,10},{10,1... | collective-permute-start | bytes 884744 | tf_op jit(solution)/shard_map/ppermute | solution.py:83
  41.1 7.9 %collective-permute-start.4 = (bf16[256,576]{0,1:T(8,128)(2,1)S(1)}, bf16[256,576]{0,1:T(8,128)(2,1)S(1)}, u32[]{:S(2)}, u32[]{:S(2)}) collective-permute-start(bf16[256,576]{0,1:T(8,128)(2,1)S(1)} %collective-permute-done.3), channel_id=1, source_target_pairs={{0,1},{1,2},{2,3},{3,4},{4,5},{5,6},{6,7},{7,0},{8,9},{9,10},{10,1... | collective-permute-start | bytes 884744 | tf_op jit(solution)/shard_map/ppermute | solution.py:83
  49.1 7.9 %collective-permute-start.5 = (bf16[256,576]{0,1:T(8,128)(2,1)S(1)}, bf16[256,576]{0,1:T(8,128)(2,1)S(1)}, u32[]{:S(2)}, u32[]{:S(2)}) collective-permute-start(bf16[256,576]{0,1:T(8,128)(2,1)S(1)} %collective-permute-done.4), channel_id=1, source_target_pairs={{0,1},{1,2},{2,3},{3,4},{4,5},{5,6},{6,7},{7,0},{8,9},{9,10},{10,1... | collective-permute-start | bytes 884744 | tf_op jit(solution)/shard_map/ppermute | solution.py:83
  57.0 7.9 %collective-permute-start.6 = (bf16[256,576]{0,1:T(8,128)(2,1)S(1)}, bf16[256,576]{0,1:T(8,128)(2,1)S(1)}, u32[]{:S(2)}, u32[]{:S(2)}) collective-permute-start(bf16[256,576]{0,1:T(8,128)(2,1)S(1)} %collective-permute-done.5), channel_id=1, source_target_pairs={{0,1},{1,2},{2,3},{3,4},{4,5},{5,6},{6,7},{7,0},{8,9},{9,10},{10,1... | collective-permute-start | bytes 884744 | tf_op jit(solution)/shard_map/ppermute | solution.py:83
  67.1 10.0 %copy-start.1 = (bf16[8,256,576]{1,2,0:T(8,128)(2,1)S(1)}, bf16[8,256,576]{1,2,0:T(8,128)(2,1)}, u32[]{:S(2)}) copy-start(bf16[8,256,576]{1,2,0:T(8,128)(2,1)} %gather_fusion) | copy-start | bytes 7077892
  67.1 10.0 %copy-start.6 = (bf16[4608,16]{0,1:T(8,128)(2,1)S(1)}, bf16[4608,16]{0,1:T(8,128)(2,1)}, u32[]{:S(2)}) copy-start(bf16[4608,16]{0,1:T(8,128)(2,1)} %param.17) | copy-start | bytes 442372
  67.1 10.0 %copy-start.8 = (bf16[16,128]{1,0:T(8,128)(2,1)S(1)}, bf16[16,128]{1,0:T(8,128)(2,1)}, u32[]{:S(2)}) copy-start(bf16[16,128]{1,0:T(8,128)(2,1)} %param.18) | copy-start | bytes 12292
  78.1 8.4 %copy-start.7 = (bf16[16,256]{1,0:T(8,128)(2,1)S(1)}, bf16[16,256]{1,0:T(8,128)(2,1)}, u32[]{:S(2)}) copy-start(bf16[16,256]{1,0:T(8,128)(2,1)} %param.16) | copy-start | bytes 24580
Sparse Core Ops, SparseCore 0:
  8.9 25.4 all-gather.5
  35.9 22.7 all-gather.3
  60.3 38.1 all-gather.7
